TPU v7x, 32 devices: a whole 2x2x4 slice. The times are simulated.
32 devices in a mesh: copy: 4 (over z), row: 4 (over x, core), col: 2 (over y).
Axes of the slice: x: 2, y: 2, z: 4, core: 2. Of those that a mesh axis runs over, the one named last changes fastest.
Arguments:
- trailing: float32 [32768, 16, 2, 128], P(('copy', 'row'), None, 'col'), parts along dimension 0, may hold values from -6 to 6
- lower_trail: float32 [64, 2, 128, 768], P(('copy', 'row'), None, None, 'col'), parts along dimension 0, may hold values from -0.09375 to 0.09375
- lower_cross: float32 [384, 384], replicated, may hold values from -0.3125 to 0.3125
- panel_inverse: float32 [2, 384, 384], replicated, may hold values from -1 to 1, as said below
- target: float32 [32768, 2, 384], P(('copy', 'row'), None, 'col'), parts along dimension 0, may hold values from -6 to 6
Outputs:
- inverse_panels: float32 [32768, 2, 384], P(('copy', 'row'), None, 'col'), parts along dimension 0
There are 4 independent parts, one for each index of `copy`. A program takes and returns all parts, laid end to end along the dimension named above; an argument that names none is the same for every part. Nothing has to cross between parts.
Inputs may be any that keep to these rules, and one draw needn't show every extreme that they name: `panel_inverse`: each of the two 384 x 384 matrices is unit lower triangular: ones on the diagonal, zeros above it.
All inputs are finite; a program needn't handle non-finite values.
Results may differ from a plain program's by a relative error of at most 0.000071.
Values sent between devices are 32-bit elements; how exact they have to be, the bound alone decides.
A program may use at most 192 MiB of HBM per device.

v0:
```python
import jax
import jax.numpy as jnp
from jax import lax
from jax.sharding import PartitionSpec as P

precise = lax.Precision.HIGHEST


def matmul(first, second):
    return jnp.dot(first, second, preferred_element_type=jnp.float32, precision=precise)


def own_columns(matrix, dim):
    share_cols = matrix.shape[dim] // lax.axis_size("col")
    return lax.dynamic_slice_in_dim(matrix, lax.axis_index("col") * share_cols, share_cols, dim)


def per_device(trailing, lower_trail, lower_cross, panel_inverse, target):
    row_count = trailing.shape[0]
    block_cols = trailing.shape[3]
    trail_flat = trailing.reshape(row_count, trailing.shape[1] * block_cols)
    span_cols = lower_trail.shape[3] * lax.axis_size("col")
    panel_cols = span_cols // 2
    relaid = lax.all_to_all(lower_trail, "col", split_axis=1, concat_axis=3, tiled=True)
    segment = lax.all_gather(relaid, "row", axis=0, tiled=True)
    block_count = segment.shape[0]
    update = matmul(trail_flat, segment.reshape(block_count * block_cols, span_cols))
    update = update.reshape(row_count, 2, panel_cols)
    right_sum = lax.psum_scatter(update[:, 1], "col", scatter_dimension=1, tiled=True)
    right_rest = lax.all_gather(target[:, 1] - right_sum, "col", axis=1, tiled=True)
    right_panel = matmul(right_rest, panel_inverse[1])
    left_sum = lax.psum_scatter(update[:, 0], "col", scatter_dimension=1, tiled=True)
    left_rest = lax.all_gather(target[:, 0] - left_sum, "col", axis=1, tiled=True)
    left_panel = matmul(left_rest - matmul(right_panel, lower_cross), panel_inverse[0])
    return own_columns(jnp.stack([left_panel, right_panel], axis=1), 2)


def solution(mesh):
    placed = (
        P(("copy", "row"), None, "col", None),
        P(("copy", "row"), None, None, "col"),
        P(),
        P(),
        P(("copy", "row"), None, "col"),
    )
    return jax.shard_map(
        per_device,
        mesh=mesh,
        in_specs=placed,
        out_specs=P(("copy", "row"), None, "col"),
        check_vma=False,
    )
```

profile of v0, /device:TPU:0, one launch (start us, length us, event | category | flops | bytes accessed | tf_op | source)
XLA Modules:
  0.0 366.6 jit_solution(11289346331029031825)
XLA Ops:
  6.5 1.9 copy.17
  8.5 23.3 %all_to_all.18 = f32[4,2,128,384]{2,3,0,1:T(8,128)S(1)} all-to-all(f32[4,2,128,384]{2,3,0,1:T(8,128)S(1)} %copy.17), channel_id=1, replica_groups=mesh['copy'=4,'row'=4,'col'=2] {'col'}, dimensions={1} | all-to-all | bytes 3145728 | tf_op jit(solution)/shard_map/all_to_all | solution.py:24
  31.7 0.1 copy.18
  31.9 1.6 copy.19
  33.5 0.5 broadcast.3
  34.1 50.0 %reduce.3 = f32[2048,16,128]{2,1,0:T(8,128)} reduce(f32[2048,16,1,128]{3,2,1,0:T(1,128)} %param.5, f32[]{:T(128)} %broadcast.3), dimensions={2}, to_apply=%param.5.reduce_sub_computation.3 | reduce | bytes 33554436 | tf_op args[0]
  84.1 18.0 %reshape.10 = f32[2048,2048,1]{1,0,2:T(8,128)} reshape(f32[2048,16,128]{2,1,0:T(8,128)} %reduce.3) | data formatting | bytes 33554432 | tf_op jit(solution)/shard_map/reshape | solution.py:21
  102.1 6.6 %copy.20 = f32[768,2048]{1,0:T(8,128)} copy(f32[768,2048]{0,1:T(8,128)} %bitcast.38) | data formatting | bytes 12582912 | tf_op jit(solution)/shard_map/dot_general | solution.py:10
  108.7 49.2 %fusion.12 = f32[2048,2,384]{2,0,1:T(8,128)S(1)} fusion(f32[2048,2048,1]{1,0,2:T(8,128)} %reshape.10, f32[2,384,2048]{2,1,0:T(8,128)} %bitcast.39), kind=kOutput, calls=%fused_computation.16 | convolution fusion | flops 38654705664 | bytes 29360128 | tf_op jit(solution)/shard_map/dot_general | solution.py:10
  157.9 3.1 slice_bitcast_fusion
  161.1 3.6 copy.27
  164.7 0.0 reduce-scatter.7.cloned.1.call-start
  164.7 3.5 copy.25
  168.3 4.1 %fusion.11 = (f32[2048,1,192]{0,2,1:T(8,128)}, f32[2048,1,192]{0,2,1:T(8,128)}) fusion(f32[2048,2,192]{0,2,1:T(8,128)} %param.9), kind=kLoop, calls=%fused_computation.15 | loop fusion | bytes 6291456 | tf_op jit(solution)/shard_map/slice | solution.py:30
  172.5 1.9 copy.30
  174.3 34.4 %reduce-scatter.9.cloned.1.call-done = f32[192,2048]{1,0:T(8,128)} async-done(((f32[384,2048]{1,0:T(8,128)}), f32[192,2048]{1,0:T(8,128)}) %reduce-scatter.9.cloned.1.call-update) | async-done | bytes 1572880
  208.7 2.8 copy.28
  211.6 3.2 bitcast_subtract_fusion
  214.7 2.8 copy.23
  217.6 2.0 copy.29
  219.6 34.8 %reduce-scatter.7.cloned.1.call-done = f32[192,2048]{1,0:T(8,128)} async-done(((f32[384,2048]{1,0:T(8,128)}), f32[192,2048]{1,0:T(8,128)}) %reduce-scatter.7.cloned.1.call-update) | async-done | bytes 1572880
  254.5 2.8 copy.26
  257.2 3.2 bitcast_subtract_fusion.1
  260.4 3.0 copy.21
  263.5 37.3 %all-gather.8.cloned.1.call-done = f32[2048,384]{0,1:T(8,128)} async-done(((f32[2048,192]{0,1:T(8,128)}), f32[2048,384]{0,1:T(8,128)}) %all-gather.8.cloned.1.call-update) | async-done | bytes 3145744 | tf_op jit(solution)/shard_map/all_gather | solution.py:30
  300.8 7.3 %fusion.7 = f32[2048,384]{0,1:T(8,128)S(1)} fusion(f32[2048,384]{0,1:T(8,128)} %all-gather.8.cloned.1.call-done, f32[2,384,384]{2,1,0:T(8,128)S(1)} %copy-done.3), kind=kOutput, calls=%fused_computation.11 | convolution fusion | flops 3623878656 | bytes 6881280 | tf_op jit(solution)/shard_map/dot_general | solution.py:10
  308.1 1.7 copy-done.1
  309.8 8.2 %fusion.13 = f32[2048,384]{1,0:T(8,128)} fusion(f32[2048,384]{0,1:T(8,128)S(1)} %fusion.7, f32[384,384]{1,0:T(8,128)S(1)} %copy-done), kind=kOutput, calls=%fused_computation.17 | convolution fusion | flops 3623878656 | bytes 6881280 | tf_op jit(solution)/shard_map/dot_general | solution.py:10
  318.0 29.2 %all-gather.6.cloned.1.call-done = f32[2048,384]{0,1:T(8,128)} async-done(((f32[2048,192]{0,1:T(8,128)}), f32[2048,384]{0,1:T(8,128)}) %all-gather.6.cloned.1.call-update) | async-done | bytes 3145744 | tf_op jit(solution)/shard_map/all_gather | solution.py:33
  347.1 3.5 copy.24
  350.7 7.5 %fusion.3 = f32[2048,1,384]{0,2,1:T(8,128)S(1)} fusion(f32[2048,384]{1,0:T(8,128)} %copy.24, f32[2048,384]{1,0:T(8,128)} %fusion.13, f32[2,384,384]{2,1,0:T(8,128)S(1)} %copy-done.3), kind=kOutput, calls=%fused_computation.7 | convolution fusion | flops 3624665088 | bytes 10027008 | tf_op jit(solution)/shard_map/dot_general | solution.py:10
  358.2 1.9 fusion
  (17 shorter events, 0.2 us)
Async XLA Ops:
  6.5 303.3 %copy-start = (f32[384,384]{1,0:T(8,128)S(1)}, f32[384,384]{1,0:T(8,128)}, u32[]{:S(2)}) copy-start(f32[384,384]{1,0:T(8,128)} %param.7) | copy-start | bytes 1769476
  6.5 95.6 %all-gather.4.cloned.1.call-start = ((), (), s32[]{:S(2)}) async-start(), calls=%async_computation.3 | async-start | bytes 7864320 | tf_op jit(solution)/shard_map/all_gather | solution.py:25
  33.5 175.2 %reduce-scatter.9.cloned.1.call-start = ((), (), s32[]{:S(2)}) async-start(), calls=%async_computation.7 | async-start | bytes 4718592
  164.7 89.8 %reduce-scatter.7.cloned.1.call-start = ((), (), s32[]{:S(2)}) async-start(), calls=%async_computation.6 | async-start | bytes 4718592
  168.3 132.5 %all-gather.8.cloned.1.call-start = ((), (), s32[]{:S(2)}) async-start(), calls=%async_computation.5 | async-start | bytes 4718592 | tf_op jit(solution)/shard_map/all_gather | solution.py:30
  217.6 129.5 %all-gather.6.cloned.1.call-start = ((), (), s32[]{:S(2)}) async-start(), calls=%async_computation.4 | async-start | bytes 4718592 | tf_op jit(solution)/shard_map/all_gather | solution.py:33
  260.4 40.4 %copy-start.3 = (f32[2,384,384]{2,1,0:T(8,128)S(1)}, f32[2,384,384]{2,1,0:T(8,128)}, u32[]{:S(2)}) copy-start(f32[2,384,384]{2,1,0:T(8,128)} %param.8) | copy-start | bytes 3538948
  308.1 1.7 copy-start.1
  350.7 7.5 %copy-start.2 = (f32[2048,384]{0,1:T(8,128)S(1)}, f32[2048,384]{0,1:T(8,128)}, u32[]{:S(2)}) copy-start(f32[2048,384]{0,1:T(8,128)} %copy-done.1) | copy-start | bytes 9437188
Sparse Core Ops, SparseCore 0:
  33.6 46.8 all-gather.3
  164.8 43.8 reduce-scatter.8
  211.0 43.4 reduce-scatter.6
  255.9 44.9 all-gather.7
  302.2 44.8 all-gather.5
where the time goes:
time: 368 us; the launch traced here: 367 us
  waiting for transfers between devices  136 us (37%)
  matrix products  72.2 us (20%)
  local copies, waits for them, and re-layouts  63.7 us (17%)
  other arithmetic  58.3 us (16%)
  blocking collectives  23.3 us (6%)
  between operations  13.2 us (4%)
    dot_general x4, matrix products, matmul(): jnp.dot(first, second, preferred_element_type=jnp.float32, precision=prec...  72.2 us
    unnamed x7, waiting for transfers between devices  69.3 us
    unnamed x1, other arithmetic  50 us
    all_gather x1, waiting for transfers between devices, per_device(): lax.all_gather(target[:, 1] - right_sum, 'col', axis=1, tiled=True)  37.3 us
    all_gather x1, waiting for transfers between devices, per_device(): lax.all_gather(target[:, 0] - left_sum, 'col', axis=1, tiled=True)  29.2 us
    all_to_all x1, blocking collectives, per_device(): lax.all_to_all(lower_trail, 'col', split_axis=1, concat_axis=3, tiled=True)  23.3 us
    unnamed x16, local copies, waits for them, and re-layouts  20.7 us
    reshape x1, local copies, waits for them, and re-layouts, per_device(): trail_flat = trailing.reshape(row_count, trailing.shape[1] * block_cols)  18 us
  transfers between devices with their start and end apart: 5, of which 4 were waited for; matrix products, arithmetic and copies ran while one was open for 31% of the time, Pallas kernels for 0%

commit v1 on v0

--- a/solution.py
+++ b/solution.py
@@ -21,7 +21,12 @@
     trail_flat = trailing.reshape(row_count, trailing.shape[1] * block_cols)
     span_cols = lower_trail.shape[3] * lax.axis_size("col")
     panel_cols = span_cols // 2
-    relaid = lax.all_to_all(lower_trail, "col", split_axis=1, concat_axis=3, tiled=True)
+    relaid = jnp.concatenate(
+        lax.all_to_all(
+            jnp.stack(jnp.split(lower_trail, lax.axis_size("col"), axis=1)), "col", 0, 0
+        ),
+        axis=3,
+    )
     segment = lax.all_gather(relaid, "row", axis=0, tiled=True)
     block_count = segment.shape[0]
     update = matmul(trail_flat, segment.reshape(block_count * block_cols, span_cols))

time: 368 us -> 384 us (1.043)
  waiting for transfers between devices: 136 us -> 212 us
  local copies, waits for them, and re-layouts: 63.7 us -> 9.96 us
  other arithmetic: 58.3 us -> 7.16 us
  matrix products: 72.2 us -> 115 us
    reduce_scatter x0 -> x2, waiting for transfers between devices: none -> 88.5 us  [the longest x1 45.7 us: per_device(): lax.psum_scatter(update[:, 1], 'col', scatter_dimension=1, tiled=True)]
    unnamed x7 -> x5, waiting for transfers between devices: 69.3 us -> 1.26 us
    unnamed x1 -> x0, other arithmetic: 50 us -> none
    all_gather x1, waiting for transfers between devices: 0.01 us -> 46.9 us  [per_device(): segment = lax.all_gather(relaid, 'row', axis=0, tiled=True)]
    dot_general x4, matrix products: 72.2 us -> 115 us  [matmul(): jnp.dot(first, second, preferred_element_type=jnp.float32, precision=prec...]
    unnamed x16 -> x8, local copies, waits for them, and re-layouts: 20.7 us -> 1.69 us
    reshape x1 -> x2, local copies, waits for them, and re-layouts: 18 us -> 3.61 us  [per_device(): jnp.concatenate(lax.all_to_all(jnp.stack(jnp.split(lower_trail, lax.axis_...]
    all_gather x1, waiting for transfers between devices: 37.3 us -> 44.5 us  [per_device(): lax.all_gather(target[:, 1] - right_sum, 'col', axis=1, tiled=True)]
  transfers between devices with their start and end apart: 5 -> 5, of which waited for: 4 -> 5; matrix products, arithmetic and copies ran while one was open for 31% -> 4% of each run, Pallas kernels for 0% -> 0%
where the time goes in v1:
time: 384 us; the launch traced here: 381 us
  waiting for transfers between devices  212 us (55%)
  matrix products  115 us (30%)
  blocking collectives  23.3 us (6%)
  between operations  13.4 us (3%)
  local copies, waits for them, and re-layouts  9.96 us (3%)
  other arithmetic  7.16 us (2%)
    dot_general x4, matrix products, matmul(): jnp.dot(first, second, preferred_element_type=jnp.float32, precision=prec...  115 us
    all_gather x1, waiting for transfers between devices, per_device(): segment = lax.all_gather(relaid, 'row', axis=0, tiled=True)  46.9 us
    reduce_scatter x1, waiting for transfers between devices, per_device(): lax.psum_scatter(update[:, 1], 'col', scatter_dimension=1, tiled=True)  45.7 us
    all_gather x1, waiting for transfers between devices, per_device(): lax.all_gather(target[:, 1] - right_sum, 'col', axis=1, tiled=True)  44.5 us
    reduce_scatter x1, waiting for transfers between devices, per_device(): lax.psum_scatter(update[:, 0], 'col', scatter_dimension=1, tiled=True)  42.8 us
    all_gather x1, waiting for transfers between devices, per_device(): lax.all_gather(target[:, 0] - left_sum, 'col', axis=1, tiled=True)  30.4 us
    all_to_all x1, blocking collectives, per_device(): lax.all_to_all(jnp.stack(jnp.split(lower_trail, lax.axis_size('col'), axi...  23.3 us
  transfers between devices with their start and end apart: 5, of which 5 were waited for; matrix products, arithmetic and copies ran while one was open for 4% of the time, Pallas kernels for 0%

profile of v1, /device:TPU:0, one launch (start us, length us, event | category | flops | bytes accessed | tf_op | source)
XLA Modules:
  0.0 380.9 jit_solution(13763871465259631258)
XLA Ops:
  6.5 0.0 copy-start
  6.5 0.0 all-gather.4.cloned.1.call-start
  6.5 1.5 slice_bitcast_fusion.3
  8.1 0.1 pad_maximum_fusion
  8.2 23.3 %all_to_all.5 = f32[2,4,1,128,384]{4,3,1,2,0:T(8,128)S(1)} all-to-all(f32[2,4,1,128,384]{4,3,1,2,0:T(8,128)S(1)} %pad_maximum_fusion), channel_id=1, replica_groups=mesh['copy'=4,'row'=4,'col'=2] {'col'}, dimensions={0} | all-to-all | bytes 3145728 | tf_op jit(solution)/shard_map/all_to_all | solution.py:25
  31.5 1.2 copy.10
  32.7 2.4 reshape.18
  35.1 0.0 all-gather.4.cloned.1.call-update
  35.1 0.0 reduce-scatter.3.cloned.1.call-start
  35.2 46.9 %all-gather.4.cloned.1.call-done = f32[16,1,128,768]{3,2,1,0:T(8,128)} async-done(((f32[4,1,128,768]{3,2,1,0:T(8,128)}), f32[16,1,128,768]{3,2,1,0:T(8,128)}) %all-gather.4.cloned.1.call-update) | async-done | bytes 6291472 | tf_op jit(solution)/shard_map/all_gather | solution.py:30
  82.1 93.6 %fusion = f32[768,2048,1]{1,0,2:T(8,128)S(1)} fusion(f32[2048,16,128]{2,1,0:T(8,128)} %bitcast.42, f32[16,1,128,768]{3,2,1,0:T(8,128)} %all-gather.4.cloned.1.call-done), kind=kOutput, calls=%fused_computation | convolution fusion | flops 38654705664 | bytes 29360128 | tf_op jit(solution)/shard_map/dot_general | solution.py:10
  175.7 3.1 slice_bitcast_fusion
  178.8 0.0 reduce-scatter.3.cloned.1.call-update
  178.9 0.0 reduce-scatter.5.cloned.1.call-start
  178.9 0.7 reduce-scatter.5.cloned.1.call-update
  179.6 0.0 all-gather.8.cloned.1.call-start
  179.6 42.8 %reduce-scatter.3.cloned.1.call-done = f32[2048,192]{0,1:T(8,128)} async-done(((f32[2048,384]{0,1:T(8,128)}), f32[2048,192]{0,1:T(8,128)}) %reduce-scatter.3.cloned.1.call-update) | async-done | bytes 1572880 | tf_op jit(solution)/shard_map/reduce_scatter | solution.py:37
  222.5 45.7 %reduce-scatter.5.cloned.1.call-done = f32[2048,192]{0,1:T(8,128)} async-done(((f32[2048,384]{0,1:T(8,128)}), f32[2048,192]{0,1:T(8,128)}) %reduce-scatter.5.cloned.1.call-update) | async-done | bytes 1572880 | tf_op jit(solution)/shard_map/reduce_scatter | solution.py:34
  268.1 5.2 %bitcast_subtract_fusion = (f32[2048,192]{0,1:T(8,128)}, f32[2048,192]{0,1:T(8,128)}) fusion(f32[2048,192]{0,1:T(8,128)} %reduce-scatter.5.cloned.1.call-done, f32[2048,2,192]{0,2,1:T(8,128)} %param.9, f32[2048,192]{0,1:T(8,128)} %reduce-scatter.3.cloned.1.call-done), kind=kLoop, calls=%fused_computation.12 | loop fusion | flops 786432 | bytes 9437184 | tf_op jit(solution)/shard_map/sub | solution.py:35
  273.3 0.0 all-gather.8.cloned.1.call-update
  273.4 0.0 all-gather.6.cloned.1.call-start
  273.4 0.5 all-gather.6.cloned.1.call-update
  273.9 44.5 %all-gather.8.cloned.1.call-done = f32[2048,384]{0,1:T(8,128)} async-done(((f32[2048,192]{0,1:T(8,128)}), f32[2048,384]{0,1:T(8,128)}) %all-gather.8.cloned.1.call-update) | async-done | bytes 3145744 | tf_op jit(solution)/shard_map/all_gather | solution.py:35
  318.4 0.0 copy-done.3
  318.4 7.3 %fusion.10 = f32[2048,384]{0,1:T(8,128)S(1)} fusion(f32[2048,384]{0,1:T(8,128)} %all-gather.8.cloned.1.call-done, f32[2,384,384]{2,1,0:T(8,128)S(1)} %copy-done.3), kind=kOutput, calls=%fused_computation.17 | convolution fusion | flops 3623878656 | bytes 6881280 | tf_op jit(solution)/shard_map/dot_general | solution.py:10
  325.8 0.0 copy-start.1
  325.8 1.7 copy-done.1
  327.4 6.9 %fusion.14 = f32[2048,384]{0,1:T(8,128)} fusion(f32[2048,384]{0,1:T(8,128)S(1)} %fusion.10, f32[384,384]{1,0:T(8,128)S(1)} %copy-done), kind=kOutput, calls=%fused_computation.21 | convolution fusion | flops 3623878656 | bytes 6881280 | tf_op jit(solution)/shard_map/dot_general | solution.py:10
  334.4 30.4 %all-gather.6.cloned.1.call-done = f32[2048,384]{0,1:T(8,128)} async-done(((f32[2048,192]{0,1:T(8,128)}), f32[2048,384]{0,1:T(8,128)}) %all-gather.6.cloned.1.call-update) | async-done | bytes 3145744 | tf_op jit(solution)/shard_map/all_gather | solution.py:38
  364.8 7.5 %fusion.6 = f32[2048,1,384]{0,2,1:T(8,128)S(1)} fusion(f32[2048,384]{0,1:T(8,128)} %all-gather.6.cloned.1.call-done, f32[2048,384]{0,1:T(8,128)} %fusion.14, f32[2,384,384]{2,1,0:T(8,128)S(1)} %copy-done.3), kind=kOutput, calls=%fused_computation.10 | convolution fusion | flops 3624665088 | bytes 10027008 | tf_op jit(solution)/shard_map/dot_general | solution.py:10
  372.3 0.0 copy-done.2
  372.3 1.9 fusion.3
  (3 shorter events, 0.0 us)
Async XLA Ops:
  6.5 320.9 %copy-start = (f32[384,384]{1,0:T(8,128)S(1)}, f32[384,384]{1,0:T(8,128)}, u32[]{:S(2)}) copy-start(f32[384,384]{1,0:T(8,128)} %param.7) | copy-start | bytes 1769476
  6.5 75.6 %all-gather.4.cloned.1.call-start = ((), (), s32[]{:S(2)}) async-start(), calls=%async_computation.3 | async-start | bytes 7864320 | tf_op jit(solution)/shard_map/all_gather | solution.py:30
  35.1 187.3 %reduce-scatter.3.cloned.1.call-start = ((), (), s32[]{:S(2)}) async-start(), calls=%async_computation.4 | async-start | bytes 4718592 | tf_op jit(solution)/shard_map/reduce_scatter | solution.py:37
  178.9 89.3 %reduce-scatter.5.cloned.1.call-start = ((), (), s32[]{:S(2)}) async-start(), calls=%async_computation.6 | async-start | bytes 4718592 | tf_op jit(solution)/shard_map/reduce_scatter | solution.py:34
  179.6 138.8 %all-gather.8.cloned.1.call-start = ((), (), s32[]{:S(2)}) async-start(), calls=%async_computation.7 | async-start | bytes 4718592 | tf_op jit(solution)/shard_map/all_gather | solution.py:35
  273.3 45.1 %copy-start.3 = (f32[2,384,384]{2,1,0:T(8,128)S(1)}, f32[2,384,384]{2,1,0:T(8,128)}, u32[]{:S(2)}) copy-start(f32[2,384,384]{2,1,0:T(8,128)} %param.8) | copy-start | bytes 3538948
  273.4 91.4 %all-gather.6.cloned.1.call-start = ((), (), s32[]{:S(2)}) async-start(), calls=%async_computation.5 | async-start | bytes 4718592 | tf_op jit(solution)/shard_map/all_gather | solution.py:38
  325.8 1.7 copy-start.1
  364.8 7.5 %copy-start.2 = (f32[2048,384]{0,1:T(8,128)S(1)}, f32[2048,384]{0,1:T(8,128)}, u32[]{:S(2)}) copy-start(f32[2048,384]{0,1:T(8,128)} %copy-done.1) | copy-start | bytes 9437188
Sparse Core Ops, SparseCore 0:
  35.2 46.8 all-gather.3
  179.0 43.4 reduce-scatter.2
  224.7 43.3 reduce-scatter.4
  273.5 44.9 all-gather.7
  319.8 44.8 all-gather.5
